TPU v7x, 128 devices: a whole 4x4x4 slice. The times are simulated.
128 devices in a mesh: fsdp: 128 (over x, z, y, core).
Axes of the slice: x: 4, y: 4, z: 4, core: 2. Of those that a mesh axis runs over, the one named last changes fastest.
Arguments:
- statistics: float32 [128, 1024, 1024], P(None, 'fsdp'), may hold values from -60 to 200, as said below
- gradient: bfloat16 [128, 1024, 1024], P(None, 'fsdp'), may hold values from -24 to 24
- block_slot: int32 [128], replicated, may hold values from 0 to 127, each once
Outputs:
- new_statistics: float32 [128, 1024, 1024], P(None, 'fsdp')
- slot_roots: float32 [128, 1024, 1024], P('fsdp')
- update: float32 [128, 1024, 1024], P(None, 'fsdp')
Inputs may be any that keep to these rules, and one draw needn't show every extreme that they name: block_slot is a permutation of 0 to 127. Every block of statistics is symmetric with all eigenvalues at least 10.
All inputs are finite; a program needn't handle non-finite values.
Results may differ from a plain program's by a relative error of at most 0.0003.
Values may be sent and summed in bfloat16 or wider, within the bound.
A program may use at most 128 MiB of HBM per device.

v0:
```python
import functools

import jax
import jax.numpy as jnp
from jax import lax
from jax.sharding import Mesh
from jax.sharding import PartitionSpec as P

ITERS = 4
FSDP = ("fsdp_0", "fsdp_1", "fsdp_2", "fsdp_3")


stat_decay = 0.95
ridge_scale = 0.001


def one_axis_at_a_time(x, axes):
    return functools.reduce(lax.psum, axes, x)


def inverse_root(matrix):
    block_width = matrix.shape[0]
    identity = jnp.eye(block_width, dtype=jnp.float32)
    frobenius = jnp.sqrt(jnp.sum(matrix * matrix))
    shrink = 2.5 / frobenius
    current = shrink * matrix
    result_root = jnp.sqrt(jnp.sqrt(shrink)) * identity
    for iteration in range(ITERS):
        factor = (5.0 * identity - current) * 0.25
        result_root = jnp.dot(result_root, factor, precision=lax.Precision.HIGHEST)
        square = jnp.dot(factor, factor, precision=lax.Precision.HIGHEST)
        fourth = jnp.dot(square, square, precision=lax.Precision.HIGHEST)
        current = jnp.dot(fourth, current, precision=lax.Precision.HIGHEST)
    return result_root


def renew_block(stat_block, grad_block):
    outer = lax.dot_general(
        grad_block, grad_block, (((1,), (1,)), ((), ())), preferred_element_type=jnp.float32
    )
    return stat_decay * stat_block + (1.0 - stat_decay) * outer


def damped_root(renewed):
    block_width = renewed.shape[0]
    diag_sum = jnp.trace(renewed)
    damped = renewed + ridge_scale * (diag_sum / block_width) * jnp.eye(
        block_width, dtype=jnp.float32
    )
    return inverse_root(damped)


def apply_root(root_block, grad_block):
    return jnp.dot(root_block, grad_block.astype(jnp.float32), precision=lax.Precision.HIGHEST)


def return_rows(blocks):
    return lax.all_to_all(blocks, FSDP, split_axis=1, concat_axis=0, tiled=True)


def body(statistics, gradient, block_slot):
    block_count = block_slot.shape[0]
    placed = (
        jnp.zeros((block_count,), jnp.int32)
        .at[block_slot]
        .set(jnp.arange(block_count, dtype=jnp.int32))
    )
    stat_rows = jnp.take(statistics, placed, axis=0)
    grad_rows = jnp.take(gradient, placed, axis=0)
    grad_sq = jnp.sum(jnp.square(gradient.astype(jnp.float32)))
    grad_total = one_axis_at_a_time(grad_sq, FSDP)
    stat_blocks = lax.all_to_all(stat_rows, FSDP, split_axis=0, concat_axis=1, tiled=True)
    grad_blocks = lax.all_to_all(grad_rows, FSDP, split_axis=0, concat_axis=1, tiled=True)
    renewed = jax.vmap(renew_block)(stat_blocks, grad_blocks)
    renewed_rows = return_rows(renewed)
    roots = jax.vmap(damped_root)(renewed)
    raw_update = jax.vmap(apply_root)(roots, grad_blocks)
    raw_sq = jnp.sum(raw_update * raw_update)
    raw_total = one_axis_at_a_time(raw_sq, FSDP)
    update_rows = lax.all_to_all(raw_update, FSDP, split_axis=1, concat_axis=0, tiled=True)
    graft_ratio = jnp.sqrt(grad_total) / jnp.sqrt(raw_total)
    new_statistics = jnp.take(renewed_rows, block_slot, axis=0)
    update = graft_ratio * jnp.take(update_rows, block_slot, axis=0)
    return (new_statistics, roots, update)


def solution(mesh):
    finer = Mesh(mesh.devices.reshape(4, 4, 4, 2), ("fsdp_0", "fsdp_1", "fsdp_2", "fsdp_3"))
    placed = (P(None, FSDP, None), P(None, FSDP, None), P())
    return jax.shard_map(
        body,
        mesh=finer,
        in_specs=placed,
        out_specs=(P(None, FSDP, None), P(FSDP, None, None), P(None, FSDP, None)),
        check_vma=False,
    )
```

profile of v0, /device:TPU:1, one launch (start us, length us, event | category | flops | bytes accessed | tf_op | source)
XLA Modules:
  0.0 515.4 jit_solution(12047565959552446908)
XLA Ops:
  6.2 11.5 %all-to-all-start.1 = ((bf16[128,8,1024]{2,1,0:T(8,128)(2,1)}), bf16[128,8,1024]{2,1,0:T(8,128)(2,1)S(1)}, u32[]{:S(2)}, u32[]{:S(2)}) async-start(bf16[128,8,1024]{2,1,0:T(8,128)(2,1)} %broadcast_select_fusion.2), calls=%async_computation.1 | async-start | bytes 4194304 | tf_op jit(solution)/shard_map/all_to_all | solution.py:73
  17.7 5.0 gather_fusion.1
  27.3 21.7 %all-to-all-done.1 = bf16[128,8,1024]{2,1,0:T(8,128)(2,1)S(1)} async-done(((bf16[128,8,1024]{2,1,0:T(8,128)(2,1)}), bf16[128,8,1024]{2,1,0:T(8,128)(2,1)S(1)}, u32[]{:S(2)}, u32[]{:S(2)}) %all-to-all-start.1) | async-done | bytes 2097184 | tf_op jit(solution)/shard_map/all_to_all | solution.py:73
  48.9 66.4 %all_to_all.42 = f32[128,8,1024]{2,1,0:T(8,128)S(1)} all-to-all(f32[128,8,1024]{2,1,0:T(8,128)} %broadcast_select_fusion.1), channel_id=1, replica_groups=mesh['fsdp_0'=4,'fsdp_1'=4,'fsdp_2'=4,'fsdp_3'=2] {'fsdp_0','fsdp_1','fs..., dimensions={0} | all-to-all | bytes 8388608 | tf_op jit(solution)/shard_map/all_to_all | solution.py:72
  115.4 5.2 %select_reduce_fusion = (f32[]{:T(128)}, f32[1024,1024]{1,0:T(8,128)}) fusion(bf16[128,8,1024]{2,1,0:T(8,128)(2,1)S(1)} %all-to-all-done.1, f32[128,8,1024]{2,1,0:T(8,128)S(1)} %all_to_all.42), kind=kOutput, calls=%fused_computation.24 | convolution fusion | flops 2153775104 | bytes 10485764 | tf_op jit(solution)/shard_map/vmap()/dot_general | solution.py:38
  125.8 20.2 %fusion.18 = f32[1024,1024]{1,0:T(8,128)} fusion(f32[]{:T(128)S(6)} %div.7, f32[1024,1024]{1,0:T(8,128)} %get-tuple-element.15, f32[]{:T(128)S(6)} %mul.97), kind=kOutput, calls=%fused_computation.32 | convolution fusion | flops 12892241920 | bytes 8388616 | tf_op jit(solution)/shard_map/vmap()/dot_general | solution.py:31
  146.1 16.7 %fusion.6 = f32[1024,1024]{1,0:T(8,128)S(1)} fusion(f32[]{:T(128)S(6)} %div.7, f32[]{:T(128)S(6)} %sqrt.19, f32[1024,1024]{1,0:T(8,128)} %get-tuple-element.15, f32[]{:T(128)S(6)} %mul.97), kind=kOutput, calls=%fused_computation.20 | convolution fusion | flops 12894339072 | bytes 8388620 | tf_op jit(solution)/shard_map/vmap()/dot_general | solution.py:30
  162.9 13.4 %fusion.73 = f32[1024,1024]{1,0:T(8,128)S(1)} fusion(f32[1024,1024]{1,0:T(8,128)S(1)} %copy-done.4), kind=kOutput, calls=%fused_computation.94 | convolution fusion | flops 12884901888 | bytes 8388608 | tf_op jit(solution)/shard_map/vmap()/dot_general | solution.py:32
  176.3 13.7 %fusion.8 = f32[1024,1024]{1,0:T(8,128)S(1)} fusion(f32[1024,1024]{1,0:T(8,128)S(1)} %fusion.73, f32[]{:T(128)S(6)} %div.7, f32[1024,1024]{1,0:T(8,128)S(1)} %copy-done, f32[]{:T(128)S(6)} %mul.97), kind=kOutput, calls=%fused_computation.26 | convolution fusion | flops 12889096192 | bytes 12582920 | tf_op jit(solution)/shard_map/vmap()/dot_general | solution.py:33
  190.0 13.7 %fusion.14 = f32[1024,1024]{1,0:T(8,128)S(1)} fusion(f32[1024,1024]{1,0:T(8,128)S(1)} %fusion.8), kind=kOutput, calls=%fused_computation.30 | convolution fusion | flops 12889096192 | bytes 8388608 | tf_op jit(solution)/shard_map/vmap()/dot_general | solution.py:31
  203.7 13.9 %fusion.16 = f32[1024,1024]{1,0:T(8,128)S(1)} fusion(f32[1024,1024]{1,0:T(8,128)S(1)} %fusion.6, f32[1024,1024]{1,0:T(8,128)S(1)} %fusion.8), kind=kOutput, calls=%fused_computation.31 | convolution fusion | flops 12889096192 | bytes 12582912 | tf_op jit(solution)/shard_map/vmap()/dot_general | solution.py:30
  217.7 13.6 %fusion.74 = f32[1024,1024]{1,0:T(8,128)S(1)} fusion(f32[1024,1024]{1,0:T(8,128)S(1)} %fusion.14), kind=kOutput, calls=%fused_computation.95 | convolution fusion | flops 12884901888 | bytes 8388608 | tf_op jit(solution)/shard_map/vmap()/dot_general | solution.py:32
  231.3 13.7 %fusion.75 = f32[1024,1024]{1,0:T(8,128)S(1)} fusion(f32[1024,1024]{1,0:T(8,128)S(1)} %fusion.74, f32[1024,1024]{1,0:T(8,128)S(1)} %fusion.8), kind=kOutput, calls=%fused_computation.96 | convolution fusion | flops 12884901888 | bytes 12582912 | tf_op jit(solution)/shard_map/vmap()/dot_general | solution.py:33
  245.0 13.9 %fusion.10 = f32[1024,1024]{1,0:T(8,128)S(1)} fusion(f32[1024,1024]{1,0:T(8,128)S(1)} %fusion.75), kind=kOutput, calls=%fused_computation.28 | convolution fusion | flops 12889096192 | bytes 8388608 | tf_op jit(solution)/shard_map/vmap()/dot_general | solution.py:31
  258.9 13.7 %fusion.12 = f32[1024,1024]{1,0:T(8,128)S(1)} fusion(f32[1024,1024]{1,0:T(8,128)S(1)} %fusion.16, f32[1024,1024]{1,0:T(8,128)S(1)} %fusion.75), kind=kOutput, calls=%fused_computation.29 | convolution fusion | flops 12889096192 | bytes 12582912 | tf_op jit(solution)/shard_map/vmap()/dot_general | solution.py:30
  272.6 13.6 %fusion.76 = f32[1024,1024]{1,0:T(8,128)S(1)} fusion(f32[1024,1024]{1,0:T(8,128)S(1)} %fusion.10), kind=kOutput, calls=%fused_computation.97 | convolution fusion | flops 12884901888 | bytes 8388608 | tf_op jit(solution)/shard_map/vmap()/dot_general | solution.py:32
  286.2 13.9 %fusion.77 = f32[1024,1024]{1,0:T(8,128)S(1)} fusion(f32[1024,1024]{1,0:T(8,128)S(1)} %fusion.76, f32[1024,1024]{1,0:T(8,128)S(1)} %fusion.75), kind=kOutput, calls=%fused_computation.98 | convolution fusion | flops 12884901888 | bytes 12582912 | tf_op jit(solution)/shard_map/vmap()/dot_general | solution.py:33
  300.1 13.7 %fusion.4 = f32[1024,1024]{1,0:T(8,128)S(1)} fusion(f32[1024,1024]{1,0:T(8,128)S(1)} %fusion.12, f32[1024,1024]{1,0:T(8,128)S(1)} %fusion.77), kind=kOutput, calls=%fused_computation.13 | convolution fusion | flops 12889096192 | bytes 12582912 | tf_op jit(solution)/shard_map/vmap()/dot_general | solution.py:30
  313.8 8.0 %multiply_reduce_fusion = (f32[]{:T(128)}, f32[1024,1024]{1,0:T(8,128)S(1)}) fusion(f32[1024,1024]{1,0:T(8,128)S(1)} %fusion.4, bf16[128,8,1024]{2,1,0:T(8,128)(2,1)S(1)} %all-to-all-done.1), kind=kOutput, calls=%fused_computation.18 | convolution fusion | flops 12886999040 | bytes 10485764 | tf_op jit(solution)/shard_map/vmap()/dot_general | solution.py:54
  321.8 6.3 %copy.7 = f32[1,1024,1024]{2,0,1:T(1,128)} copy(f32[1,1024,1024]{2,1,0:T(8,128)S(1)} %bitcast.38) | data formatting | bytes 8388608 | tf_op jit(solution)/shard_map/vmap()/dot_general | solution.py:54
  328.1 6.6 %all-to-all-start.3 = ((f32[1,1024,1024]{2,0,1:T(1,128)}), f32[1,1024,1024]{2,0,1:T(1,128)}, u32[]{:S(2)}, u32[]{:S(2)}) async-start(f32[1,1024,1024]{2,0,1:T(1,128)} %copy.7), calls=%async_computation.3 | async-start | bytes 8388608 | tf_op jit(solution)/shard_map/all_to_all | solution.py:80
  334.7 8.5 %copy.6 = f32[1,1024,1024]{2,0,1:T(1,128)} copy(f32[1,1024,1024]{2,1,0:T(8,128)} %bitcast.35) | data formatting | bytes 8388608 | tf_op jit(solution)/shard_map/vmap()/add | solution.py:41
  343.1 49.8 %all-to-all-done.3 = f32[1,1024,1024]{2,0,1:T(1,128)} async-done(((f32[1,1024,1024]{2,0,1:T(1,128)}), f32[1,1024,1024]{2,0,1:T(1,128)}, u32[]{:S(2)}, u32[]{:S(2)}) %all-to-all-start.3) | async-done | bytes 4194336 | tf_op jit(solution)/shard_map/all_to_all | solution.py:80
  393.0 8.2 %all-to-all-start.2 = ((f32[1,1024,1024]{2,0,1:T(1,128)}), f32[1,1024,1024]{2,0,1:T(1,128)}, u32[]{:S(2)}, u32[]{:S(2)}) async-start(f32[1,1024,1024]{2,0,1:T(1,128)} %copy.6), calls=%async_computation.2 | async-start | bytes 8388608 | tf_op jit(solution)/shard_map/all_to_all | solution.py:58
  402.9 52.5 %all-reduce.2 = (f32[]{:T(128)}, f32[]{:T(128)}) all-reduce(f32[]{:T(128)} %multiply_reduce_fusion.1, f32[]{:T(128)} %get-tuple-element.16), channel_id=1, replica_groups=mesh['fsdp_0'=4,'fsdp_1'=4,'fsdp_2'=4,'fsdp_3'=2] {'fsdp_0'}, use_global_device_ids=true, to_apply=%region_4.6 | all-reduce | flops 2 | bytes 16 | tf_op jit(solution)/shard_map/psum | solution.py:18
  455.4 11.7 %all-reduce.1 = (f32[]{:T(128)}, f32[]{:T(128)}) all-reduce(f32[]{:T(128)} %get-tuple-element.8, f32[]{:T(128)} %get-tuple-element.9), channel_id=1, replica_groups=mesh['fsdp_0'=4,'fsdp_1'=4,'fsdp_2'=4,'fsdp_3'=2] {'fsdp_1'}, use_global_device_ids=true, to_apply=%region_5.7 | all-reduce | flops 2 | bytes 16 | tf_op jit(solution)/shard_map/psum | solution.py:18
  467.1 10.2 %all-reduce = (f32[]{:T(128)}, f32[]{:T(128)}) all-reduce(f32[]{:T(128)} %get-tuple-element.6, f32[]{:T(128)} %get-tuple-element.7), channel_id=1, replica_groups=mesh['fsdp_0'=4,'fsdp_1'=4,'fsdp_2'=4,'fsdp_3'=2] {'fsdp_2'}, use_global_device_ids=true, to_apply=%region_6.8 | all-reduce | flops 2 | bytes 16 | tf_op jit(solution)/shard_map/psum | solution.py:18
  477.3 8.6 %all-reduce.3 = (f32[]{:T(128)}, f32[]{:T(128)}) all-reduce(f32[]{:T(128)} %get-tuple-element.4, f32[]{:T(128)} %get-tuple-element.5), channel_id=1, replica_groups=mesh['fsdp_0'=4,'fsdp_1'=4,'fsdp_2'=4,'fsdp_3'=2] {'fsdp_3'}, use_global_device_ids=true, to_apply=%region_7.9 | all-reduce | flops 2 | bytes 16 | tf_op jit(solution)/shard_map/psum | solution.py:18
  487.3 5.2 %copy.12 = f32[1,1024,1024]{2,1,0:T(8,128)} copy(f32[1,1024,1024]{2,0,1:T(1,128)} %all-to-all-done.3) | data formatting | bytes 8388608
  492.5 5.0 gather_fusion.3
  497.6 5.2 %copy.13 = f32[1,1024,1024]{2,1,0:T(8,128)} copy(f32[1,1024,1024]{2,0,1:T(1,128)} %all-to-all-done.2) | data formatting | bytes 8388608
  507.7 7.5 %select_multiply_fusion = (f32[128,8,1024]{2,1,0:T(8,128)}, f32[128,8,1024]{2,1,0:T(8,128)}) fusion(f32[128,8,1024]{2,1,0:T(8,128)} %gather_fusion.3, f32[]{:T(128)S(6)} %div.8, pred[128]{0:T(512)(128)(4,1)S(1)} %compare_and_fusion, f32[128,8,1024]{2,1,0:T(8,128)} %gather_fusion.2), kind=kLoop, calls=%fused_computation.17 | loop fusion | flops 3145728 | bytes 16777348 | tf_op jit(solution)/shard_map/mul | solution.py:83
  (25 shorter events, 20.6 us)
Async XLA Ops:
  6.2 42.8 %all-to-all-start.1 = ((bf16[128,8,1024]{2,1,0:T(8,128)(2,1)}), bf16[128,8,1024]{2,1,0:T(8,128)(2,1)S(1)}, u32[]{:S(2)}, u32[]{:S(2)}) async-start(bf16[128,8,1024]{2,1,0:T(8,128)(2,1)} %broadcast_select_fusion.2), calls=%async_computation.1 | async-start | bytes 4194304 | tf_op jit(solution)/shard_map/all_to_all | solution.py:73
  146.1 16.8 %copy-start.4 = (f32[1024,1024]{1,0:T(8,128)S(1)}, f32[1024,1024]{1,0:T(8,128)}, u32[]{:S(2)}) copy-start(f32[1024,1024]{1,0:T(8,128)} %fusion.18) | copy-start | bytes 12582916
  162.9 13.4 %copy-start = (f32[1024,1024]{1,0:T(8,128)S(1)}, f32[1024,1024]{1,0:T(8,128)}, u32[]{:S(2)}) copy-start(f32[1024,1024]{1,0:T(8,128)} %get-tuple-element.15) | copy-start | bytes 12582916
  313.7 8.0 %copy-start.3 = (f32[1024,1024]{1,0:T(8,128)}, f32[1024,1024]{1,0:T(8,128)S(1)}, u32[]{:S(2)}) copy-start(f32[1024,1024]{1,0:T(8,128)S(1)} %fusion.4) | copy-start | bytes 12582916
  328.1 64.9 %all-to-all-start.3 = ((f32[1,1024,1024]{2,0,1:T(1,128)}), f32[1,1024,1024]{2,0,1:T(1,128)}, u32[]{:S(2)}, u32[]{:S(2)}) async-start(f32[1,1024,1024]{2,0,1:T(1,128)} %copy.7), calls=%async_computation.3 | async-start | bytes 8388608 | tf_op jit(solution)/shard_map/all_to_all | solution.py:80
  343.1 58.1 %copy-start.2 = (s32[128]{0:T(128)S(1)}, s32[128]{0:T(128)}, u32[]{:S(2)}) copy-start(s32[128]{0:T(128)} %param.7) | copy-start | bytes 1540
  343.1 58.1 %copy-start.1 = (bf16[128,8,1024]{2,1,0:T(8,128)(2,1)S(1)}, bf16[128,8,1024]{2,1,0:T(8,128)(2,1)}, u32[]{:S(2)}) copy-start(bf16[128,8,1024]{2,1,0:T(8,128)(2,1)} %param.6) | copy-start | bytes 6291460
  393.0 104.6 %all-to-all-start.2 = ((f32[1,1024,1024]{2,0,1:T(1,128)}), f32[1,1024,1024]{2,0,1:T(1,128)}, u32[]{:S(2)}, u32[]{:S(2)}) async-start(f32[1,1024,1024]{2,0,1:T(1,128)} %copy.6), calls=%async_computation.2 | async-start | bytes 8388608 | tf_op jit(solution)/shard_map/all_to_all | solution.py:58
where the time goes:
time: 519 us; the launch traced here: 515 us
  matrix products  201 us (39%)
  blocking collectives  149 us (29%)
  waiting for transfers between devices  71.5 us (14%)
  local copies, waits for them, and re-layouts  43.4 us (8%)
  starting transfers between devices  26.3 us (5%)
  other arithmetic  19.9 us (4%)
    psum x4, blocking collectives, one_axis_at_a_time(): return functools.reduce(lax.psum, axes, x)  83 us
    all_to_all x1, blocking collectives, body(): lax.all_to_all(stat_rows, FSDP, split_axis=0, concat_axis=1, tiled=True)  66.4 us
    dot_general x4, matrix products, inverse_root(): result_root = jnp.dot(result_root, factor, precision=lax.Precision.HIGHEST)  58 us
    all_to_all x1, waiting for transfers between devices, body(): lax.all_to_all(raw_update, FSDP, split_axis=1, concat_axis=0, tiled=True)  49.8 us
    dot_general x3, matrix products, inverse_root(): square = jnp.dot(factor, factor, precision=lax.Precision.HIGHEST)  47.9 us
    dot_general x3, matrix products, inverse_root(): current = jnp.dot(fourth, current, precision=lax.Precision.HIGHEST)  41.2 us
    dot_general x3, matrix products, inverse_root(): fourth = jnp.dot(square, square, precision=lax.Precision.HIGHEST)  40.7 us
    all_to_all x1, waiting for transfers between devices, body(): lax.all_to_all(grad_rows, FSDP, split_axis=0, concat_axis=1, tiled=True)  21.7 us
  transfers between devices with their start and end apart: 3, of which 2 were waited for; matrix products, arithmetic and copies ran while one was open for 6% of the time, Pallas kernels for 0%

commit v1 on v0

v1 whole, which is shorter than its diff:
```python
import itertools

import jax
import jax.numpy as jnp
from jax import lax
from jax.experimental import pallas as pl
from jax.experimental.pallas import tpu as pltpu
from jax.sharding import PartitionSpec as P

N = 128
B = 1024
ROWS = 8
AXIS = "fsdp"
MESH = pl.DeviceIdType.MESH
F32 = jnp.float32
BF16 = jnp.bfloat16
I16 = jnp.int16
I32 = jnp.int32

STAT_DECAY = 0.95
RIDGE = 0.001
STAT_MAX = 200.0
TOP = 32760.0
PANEL = 256
PANELS = B // PANEL
TINY = 1e-30

CHIPS = [o for o in itertools.product(range(4), repeat=3) if any(o)]
HOPS = (0, 1, 2, 1)
FAR_FIRST = sorted(CHIPS, key=lambda o: -sum(HOPS[k] for k in o))
ROUND = [((2, 1, 3, 0)[j % 4], (5 * j + 3) % 16 // 4, (5 * j + 3) % 4) for j in range(16)]


def quarter_code(x, inverse_max):
    unit = x * inverse_max
    a = jnp.abs(unit) + TINY
    r = lax.rsqrt(a)
    s = lax.rsqrt(a * r)
    return jnp.round(unit * r * s * TOP).astype(I32).astype(I16)


def quarter_value(q, top_to_value):
    y = q.astype(I32).astype(F32)
    return (y * y) * (y * jnp.abs(y)) * top_to_value


def half_code(x, scale):
    return jnp.round(x * lax.rsqrt(jnp.abs(x) + TINY) * scale).astype(I32).astype(I16)


def half_value(q, scale):
    y = q.astype(I32).astype(F32)
    return y * jnp.abs(y) * scale


def eye_block():
    return (lax.broadcasted_iota(I32, (128, 128), 0) == lax.broadcasted_iota(I32, (128, 128), 1)).astype(F32)


def product(a, b):
    return jnp.dot(a, b, preferred_element_type=F32)


def below(p):
    return slice(PANEL * p, PANEL * (p + 1)), slice(PANEL * p, B)


def mirror(p, value, put):
    rows, cols = below(p)
    put(rows, cols, value)
    if p + 1 < PANELS:
        put(slice(PANEL * (p + 1), B), rows, value[:, PANEL:].T)


def put_bf16(ref):
    def put(rows, cols, value):
        ref[rows, cols] = value.astype(BF16)

    return put


def put_split(high, low):
    def put(rows, cols, value):
        hi = value.astype(BF16)
        high[rows, cols] = hi
        low[rows, cols] = (value - hi.astype(F32)).astype(BF16)

    return put


def exchange_kernel(
    slot_hbm, stat_hbm, grad_hbm, stat, root, outer_in, raw_in, misc_in,
    slots, placed_row, placed, gin, gsend, ssend, grecv, srecv, gm, nf, vf, nb, nl, sb, zb, vb, code, msend,
    load_p, load_g, load_s, g_out, g_in, s_out, s_in, e_out, e_in, o_out, o_in, r_out, r_in, m_out, m_in,
):
    sf = root
    me = lax.axis_index(AXIS)
    core = lax.rem(me, 2)
    sibling = me + 1 - 2 * core
    y = lax.rem(me // 2, 4)
    z = lax.rem(me // 8, 4)
    x = me // 32
    block_row = me // 16
    high = me // 64
    bit = lax.rem(me // 2, 2)
    at_x = [lax.rem(x + k, 4) * 32 for k in range(4)]
    at_z = [lax.rem(z + k, 4) * 8 for k in range(4)]
    at_y = [lax.rem(y + k, 4) * 2 for k in range(4)]

    def send(src, dst, out_sem, in_sem, target):
        pltpu.make_async_remote_copy(
            src_ref=src, dst_ref=dst, send_sem=out_sem, recv_sem=in_sem,
            device_id={AXIS: target}, device_id_type=MESH,
        ).start()

    def to_chips(cores, go):
        def step(i, carry):
            for kx, kz, ky in ROUND:
                chip = lax.rem(x + kx + i, 4) * 32 + at_z[kz] + at_y[ky]
                for c in cores:
                    if kz == 0 and ky == 0:
                        pl.when(chip + c != me)(lambda: go(chip + c))
                    else:
                        go(chip + c)
            return carry

        lax.fori_loop(0, 4, step, 0)

    barrier = pltpu.get_barrier_semaphore()
    get_p = pltpu.make_async_copy(slot_hbm, slots.at[0], load_p)
    get_g = pltpu.make_async_copy(grad_hbm, gin, load_g)
    get_s = pltpu.make_async_copy(stat_hbm, stat, load_s)
    get_p.start()
    get_g.start()
    get_s.start()

    with jax.named_scope("greet"):
        for o in FAR_FIRST:
            for c in (0, 1):
                other = at_x[o[0]] + at_z[o[1]] + at_y[o[2]] + c
                pl.semaphore_signal(barrier, inc=1, device_id={AXIS: other}, device_id_type=MESH)
        pl.semaphore_signal(barrier, inc=1, device_id={AXIS: sibling}, device_id_type=MESH)

    with jax.named_scope("placed"):
        get_p.wait()
        down = jnp.broadcast_to(slots[...], (128, 128)).T
        hit = down == lax.broadcasted_iota(I32, (128, 128), 1)
        placed_row[...] = jnp.max(
            jnp.where(hit, lax.broadcasted_iota(I32, (128, 128), 0), 0), axis=0, keepdims=True
        )
        put_p = pltpu.make_async_copy(placed_row, placed, load_p)
        put_p.start()
        get_g.wait()
        put_p.wait()

    def pack_g(s, carry):
        gsend[s] = gin[placed[0, s]]
        return carry

    with jax.named_scope("pack_g"):
        lax.fori_loop(0, N, pack_g, 0, unroll=4)
    get_s.wait()
    stat_scale = TOP / (STAT_MAX**0.5)

    def pack_s(group):
        def step(i, carry):
            s = 2 * i + group
            b = placed[0, s]
            for j in range(5):
                column = pl.multiple_of(lax.rem(block_row + j, 8) * 128, 128)
                ssend[s, :, 128 * j : 128 * (j + 1)] = half_code(stat[b, :, pl.ds(column, 128)], stat_scale)
            return carry

        with jax.named_scope("pack_s"):
            lax.fori_loop(0, N // 2, step, 0, unroll=4)

    with jax.named_scope("wait_barrier"):
        pl.semaphore_wait(barrier, N - 1)

    def send_g(target, half):
        cols = pl.ds(512 * half, 512)
        send(gsend.at[target, :, cols], grecv.at[me, :, cols], g_out, g_in, target)

    def send_s(target):
        send(ssend.at[target, :, pl.ds(0, 512)], srecv.at[me, :, pl.ds(0, 512)], s_out, s_in, target)

        @pl.when(lax.rem(target // 2, 2) == high)
        def _():
            send(ssend.at[target, :, pl.ds(512, 128)], srecv.at[me, :, pl.ds(512, 128)], e_out, e_in, target)

    for group in (0, 1):
        with jax.named_scope("send_g"):
            for half in (0, 1):
                to_chips((group,), lambda target: send_g(target, half))
        pack_s(group)
        with jax.named_scope("send_s"):
            to_chips((group,), send_s)

    grecv[me] = gsend[me]
    srecv[me] = ssend[me]

    with jax.named_scope("wait_g"):
        pltpu.make_async_copy(gsend.at[pl.ds(0, N - 1)], grecv.at[pl.ds(0, N - 1)], g_in).wait()

    def unpack_g(p, carry):
        gm[pl.ds(p * PANEL, PANEL), :] = grecv[pl.ds(p * 32, 32)].reshape(PANEL, B)
        return carry

    lane = lax.broadcasted_iota(I32, (1, 128), 1)

    def put_nf(rows, cols, value):
        nf[rows, cols] = value

    def outer_product(p):
        rows, cols = below(p)
        outer = lax.dot_general(gm[rows, :], gm[cols, :], (((1,), (1,)), ((), ())), preferred_element_type=F32)
        mirror(p, outer * (1.0 - STAT_DECAY), put_nf)

    def outer_panel(p, tops):
        rows = pl.ds(p * PANEL, PANEL)
        outer = nf[rows, :]
        top = jnp.maximum(jnp.max(jnp.abs(outer), keepdims=True), TINY)
        code[pl.ds(p * 32, 32)] = quarter_code(outer, 1.0 / top).reshape(32, ROWS, B)
        return jnp.where(lane == p, top, tops)

    with jax.named_scope("outer"):
        lax.fori_loop(0, PANELS, unpack_g, 0)
        for p in range(PANELS):
            outer_product(p)
    with jax.named_scope("outer_code"):
        outer_tops = lax.fori_loop(0, PANELS, outer_panel, jnp.zeros((1, 128), F32))

    eye = eye_block()

    def diagonal(i):
        span = pl.ds(pl.multiple_of(i * 128, 128), 128)
        return span, nf[span, span]

    def trace_step(i, total):
        return total + diagonal(i)[1] * eye

    zeros = jnp.zeros((128, 128), F32)
    grad_sq = jnp.sum(lax.fori_loop(0, 8, trace_step, zeros), keepdims=True) / (1.0 - STAT_DECAY)

    def wait_extra(count, out):
        part = pl.ds(0, count)
        pltpu.make_async_copy(
            ssend.at[part, :, pl.ds(512, 128)], srecv.at[part, :, pl.ds(512, 128)], e_out if out else e_in
        ).wait()

    def wait_extras(out):
        @pl.when(bit == high)
        def _():
            wait_extra(N // 2 - 1, out)

        @pl.when(bit != high)
        def _():
            wait_extra(N // 2, out)

    with jax.named_scope("wait_s"):
        pltpu.make_async_copy(
            ssend.at[pl.ds(0, N - 1), :, pl.ds(0, 512)], srecv.at[pl.ds(0, N - 1), :, pl.ds(0, 512)], s_in
        ).wait()
        wait_extras(False)

    stat_value = STAT_DECAY / stat_scale**2
    put_n = put_split(nb, nl)

    def add_tile(i, j, square, own):
        other = lax.rem(i + j, 8)
        tile = half_value(srecv[pl.ds(i * 16, 16), :, 128 * j : 128 * (j + 1)], stat_value).reshape(128, 128)
        rows = pl.ds(pl.multiple_of(i * 128, 128), 128)
        cols = pl.ds(pl.multiple_of(other * 128, 128), 128)
        value = nf[rows, cols] + tile
        nf[rows, cols] = value
        put_n(rows, cols, value)
        if own:
            return square + value * value
        mirrored = value.T
        nf[cols, rows] = mirrored
        put_n(cols, rows, mirrored)
        return square + 2.0 * (value * value)

    def tiles(i, square):
        for j in range(4):
            square = add_tile(i, j, square, j == 0)
        return square

    with jax.named_scope("tiles"):
        square = lax.fori_loop(0, 8, tiles, zeros)
        square = lax.fori_loop(0, 4, lambda i, acc: add_tile(i + 4 * bit, 4, acc, False), square)
        total_sq = jnp.sum(square, keepdims=True)
        trace = jnp.sum(lax.fori_loop(0, 8, trace_step, zeros), keepdims=True)
        mean = trace * (1.0 / B)
        ridge = RIDGE * mean
        total_sq = total_sq + 2.0 * ridge * trace + ridge * ridge * float(B)
        shrink = 2.5 * lax.rsqrt(total_sq)
        root_scale = lax.rsqrt(lax.rsqrt(shrink))

        def center(i, carry):
            span, value = diagonal(i)
            value = value - eye * mean
            nf[span, span] = value
            put_n(span, span, value)
            return carry

        lax.fori_loop(0, 8, center, 0)

    def send_outer():
        for half in (0, 1):
            cols = pl.ds(512 * half, 512)
            to_chips(
                (0, 1), lambda target: send(code.at[target, :, cols], outer_in.at[me, :, cols], o_out, o_in, target)
            )

    def iterate(first, k, mu, scale_y, v_unit):
        phi = (5.0 - mu) * 0.25
        phi2 = phi * phi
        phi3 = phi2 * phi
        phi4 = phi2 * phi2
        quarter_y = scale_y * 0.25
        quarter_v = v_unit * 0.25
        with jax.named_scope("square"):
            for p in range(PANELS):
                rows, cols = below(p)
                hi = nb[rows, :]
                s = product(hi, nb[:, cols]) + product(hi, nl[:, cols]) + product(nl[rows, :], nb[:, cols])
                if first:
                    s = s * (shrink * shrink)
                    vf[rows, cols] = nf[rows, cols] * (shrink * -0.25)
                    vb[1, rows, :] = hi
                else:
                    vn = product(vb[k, rows, :], nb[:, cols])
                    v = vf[rows, cols] * phi - nf[rows, cols] * quarter_y - vn * quarter_v
                    vf[rows, cols] = v
                    mirror(p, v, put_bf16(vb.at[1 - k]))
                sf[rows, cols] = s
                mirror(p, s, put_bf16(sb))
        n_n = phi4 - mu * phi3
        n_s = 0.375 * mu * phi2 - phi3
        n_t = 0.375 * phi2 - mu * phi * (1.0 / 16.0)
        z_s = mu * (1.0 / 256.0) - phi * (1.0 / 16.0)
        z_t = 1.0 / 256.0
        if first:
            n_n, n_t, z_t = n_n * shrink, n_t * shrink, z_t * shrink
        with jax.named_scope("cube"):
            for p in range(PANELS):
                rows, cols = below(p)
                t = product(sb[rows, :], nb[:, cols])
                s = sf[rows, cols]
                nf[rows, cols] = nf[rows, cols] * n_n + s * n_s + t * n_t
                mirror(p, s * z_s + t * z_t, put_bf16(zb))
        with jax.named_scope("next"):
            for p in range(PANELS):
                rows, cols = below(p)
                n = nf[rows, cols] + product(sb[rows, :], zb[:, cols])
                nf[rows, cols] = n
                mirror(p, n, put_n)
        return phi4 * mu, scale_y * phi

    one = jnp.ones((1, 1), F32)
    mu, scale_y = iterate(True, 0, shrink * mean * (1.0 + RIDGE), one, one)
    with jax.named_scope("send_outer"):
        send_outer()
        outer_in[me] = code[me]

    def later(k, carry):
        mu, scale_y, v_unit = carry
        mu, scale_y = iterate(False, lax.rem(k, 2), mu, scale_y, v_unit)
        return mu, scale_y, one

    mu, scale_y, _ = lax.fori_loop(1, 3, later, (mu, scale_y, shrink * -0.25))
    phi = (5.0 - mu) * 0.25
    diag_root = root_scale * scale_y * phi
    put_raw = put_split(sb, zb)

    def put_root(rows, cols, value):
        root[rows, cols] = value
        put_raw(rows, cols, value)

    def root_panel(p):
        rows, cols = below(p)
        v = vf[rows, cols] * phi - nf[rows, cols] * (scale_y * 0.25) - product(vb[1, rows, :], nb[:, cols]) * 0.25
        mirror(p, v * root_scale, put_root)

    def root_diagonal(i, carry):
        span = pl.ds(pl.multiple_of(i * 128, 128), 128)
        put_root(span, span, root[span, span] + eye * diag_root)
        return carry

    with jax.named_scope("root"):
        for p in range(PANELS):
            root_panel(p)
        lax.fori_loop(0, 8, root_diagonal, 0)

    front = pl.ds(0, N - 1)
    pltpu.make_async_copy(code.at[front], outer_in.at[front], o_out).wait()

    def raw_product(p):
        rows = pl.ds(p * PANEL, PANEL)
        raw = product(sb[rows, :], gm[...]) + product(zb[rows, :], gm[...])
        vf[rows, :] = raw
        return jnp.sum(raw * raw, keepdims=True), jnp.maximum(jnp.max(jnp.abs(raw), keepdims=True), TINY)

    def raw_send(p, top):
        rows = pl.ds(p * PANEL, PANEL)
        code[pl.ds(p * 32, 32)] = quarter_code(vf[rows, :], 1.0 / top).reshape(32, ROWS, B)
        for j in range(16):
            k = (5 * j + 3) % 16
            for half in (0, 1):
                for c in (0, 1):
                    cols = pl.ds(512 * half, 512)
                    target = p * 32 + at_z[k // 4] + at_y[k % 4] + c

                    def go():
                        send(code.at[target, :, cols], raw_in.at[me, :, cols], r_out, r_in, target)

                    if k == 0:
                        pl.when(target != me)(go)
                    else:
                        go()

    def panel_at(i):
        half = i // 2
        return lax.rem(x + 2 + half - lax.rem(i, 2) * (1 + 2 * half), 4)

    def raw_panel(i, carry):
        raw_sq, top, tops = carry
        p = panel_at(i)
        more, later = raw_product(p)
        raw_send(panel_at(i - 1), top)
        return raw_sq + more, later, jnp.where(lane == p, later, tops)

    with jax.named_scope("raw"):
        raw_sq, top = raw_product(panel_at(0))
        raw_sq, top, raw_tops = lax.fori_loop(
            1, PANELS, raw_panel, (raw_sq, top, jnp.where(lane == panel_at(0), top, 0.0))
        )
        raw_send(panel_at(PANELS - 1), top)

    tops = (raw_tops + pltpu.roll(outer_tops, 4, 1)) * (1.0 / TOP**4)
    msend[...] = tops + jnp.where(lane == 8, grad_sq, 0.0) + jnp.where(lane == 9, raw_sq, 0.0)
    with jax.named_scope("send_m"):
        to_chips((0, 1), lambda target: send(msend, misc_in.at[me], m_out, m_in, target))
    misc_in[me] = msend[...]
    raw_in[me] = code[me]

    with jax.named_scope("wait_out"):
        pltpu.make_async_copy(gsend.at[front], grecv.at[front], g_out).wait()
        pltpu.make_async_copy(ssend.at[front, :, pl.ds(0, 512)], srecv.at[front, :, pl.ds(0, 512)], s_out).wait()
        wait_extras(True)
        pltpu.make_async_copy(code.at[front], raw_in.at[front], r_out).wait()
        pltpu.make_async_copy(misc_in.at[front], misc_in.at[front], m_out).wait()
    with jax.named_scope("wait_o"):
        pltpu.make_async_copy(code.at[front], outer_in.at[front], o_in).wait()
    with jax.named_scope("wait_r"):
        pltpu.make_async_copy(code.at[front], raw_in.at[front], r_in).wait()
        pltpu.make_async_copy(misc_in.at[front], misc_in.at[front], m_in).wait()


def output_kernel(
    slot, stat, root, outer, raw, misc, new_out, root_out, update_out, nbuf, tbuf, oscale, rscale, root_sem, out_sems
):
    put_root = pltpu.make_async_copy(root, root_out.at[0], root_sem)
    put_root.start()
    panel = lax.axis_index(AXIS) // 32
    lane = lax.broadcasted_iota(I32, (1, 1, 128), 2)

    def pick(v, at):
        return jnp.sum(jnp.where(lane == at, v, 0.0), axis=2, keepdims=True)

    values = misc[...]
    totals = jnp.sum(values, axis=0, keepdims=True)
    graft = jnp.sqrt(pick(totals, 8)) / jnp.sqrt(pick(totals, 9))
    rscale[...] = jnp.broadcast_to(pick(values, panel) * graft, (N, 1, 128))
    oscale[...] = jnp.broadcast_to(pick(values, panel + 4), (N, 1, 128))
    step = 8

    def chunk(i, carry):
        part = pl.ds(i * step, step)
        for j in range(step):
            b = i * step + j
            s = slot[b]
            o_value = oscale[s]
            r_value = rscale[s]
            for c in range(8):
                cols = slice(128 * c, 128 * (c + 1))
                nbuf[b, :, cols] = stat[b, :, cols] * STAT_DECAY + quarter_value(outer[s, :, cols], o_value)
                tbuf[b, :, cols] = quarter_value(raw[s, :, cols], r_value)
        pltpu.make_async_copy(nbuf.at[part], new_out.at[part], out_sems.at[0, i]).start()
        pltpu.make_async_copy(tbuf.at[part], update_out.at[part], out_sems.at[1, i]).start()
        return carry

    lax.fori_loop(0, N // step, chunk, 0)
    for i in range(N // step):
        part = pl.ds(i * step, step)
        pltpu.make_async_copy(nbuf.at[part], new_out.at[part], out_sems.at[0, i]).wait()
        pltpu.make_async_copy(tbuf.at[part], update_out.at[part], out_sems.at[1, i]).wait()
    put_root.wait()


def body(statistics, gradient, block_slot):
    in_hbm = pl.BlockSpec(memory_space=pltpu.HBM)
    smem = pl.BlockSpec(memory_space=pltpu.SMEM)
    vmem = pl.BlockSpec(memory_space=pltpu.VMEM)
    dma = pltpu.SemaphoreType.DMA
    V = pltpu.VMEM
    statistics = pltpu.with_memory_space_constraint(statistics, pltpu.HBM)
    gradient = pltpu.with_memory_space_constraint(gradient, pltpu.HBM)
    block_slot = pltpu.with_memory_space_constraint(block_slot, pltpu.HBM)
    stat, root, outer_rows, raw_rows, misc = pl.pallas_call(
        exchange_kernel,
        out_shape=(
            jax.ShapeDtypeStruct((N, ROWS, B), F32),
            jax.ShapeDtypeStruct((B, B), F32),
            jax.ShapeDtypeStruct((N, ROWS, B), I16),
            jax.ShapeDtypeStruct((N, ROWS, B), I16),
            jax.ShapeDtypeStruct((N, 1, 128), F32),
        ),
        in_specs=[in_hbm, in_hbm, in_hbm],
        out_specs=(vmem,) * 5,
        scratch_shapes=[
            V((1, 128), I32), V((1, 128), I32), pltpu.SMEM((1, 128), I32),
            V((N, ROWS, B), BF16), V((N, ROWS, B), BF16), V((N, ROWS, 640), I16),
            V((N, ROWS, B), BF16), V((N, ROWS, 640), I16), V((B, B), BF16),
            V((B, B), F32), V((B, B), F32),
            V((B, B), BF16), V((B, B), BF16), V((B, B), BF16), V((B, B), BF16), V((2, B, B), BF16),
            V((N, ROWS, B), I16), V((1, 128), F32),
        ]
        + [dma] * 15,
        compiler_params=pltpu.CompilerParams(
            collective_id=0, has_side_effects=True, vmem_limit_bytes=41 * 1024 * 1024
        ),
        name="exchange",
    )(block_slot, statistics, gradient)
    return pl.pallas_call(
        output_kernel,
        out_shape=(
            jax.ShapeDtypeStruct((N, ROWS, B), F32),
            jax.ShapeDtypeStruct((1, B, B), F32),
            jax.ShapeDtypeStruct((N, ROWS, B), F32),
        ),
        in_specs=[smem, vmem, vmem, vmem, vmem, vmem],
        out_specs=(in_hbm, in_hbm, in_hbm),
        scratch_shapes=[
            V((N, ROWS, B), F32), V((N, ROWS, B), F32), V((N, 1, 128), F32), V((N, 1, 128), F32), dma, dma((2, 16)),
        ],
        compiler_params=pltpu.CompilerParams(vmem_limit_bytes=16 * 1024 * 1024),
        name="outputs",
    )(block_slot, stat, root, outer_rows, raw_rows, misc)


def solution(mesh):
    rows = P(None, AXIS, None)
    return jax.shard_map(
        body, mesh=mesh, in_specs=(rows, rows, P()), out_specs=(rows, P(AXIS, None, None), rows), check_vma=False
    )
```

time: 519 us -> 115 us (0.22)
  matrix products: 201 us -> 0 us
  blocking collectives: 149 us -> 0 us
  Pallas kernels: 0 us -> 114 us
  waiting for transfers between devices: 71.5 us -> 0 us
  local copies, waits for them, and re-layouts: 43.4 us -> 0 us
  starting transfers between devices: 26.3 us -> 0 us
  other arithmetic: 19.9 us -> 0 us
    dot_general x15 -> x0, matrix products: 201 us -> none  [the longest x4 58 us: inverse_root(): result_root = jnp.dot(result_root, factor, precision=lax.Precision.HIGHEST)]
    pallas_call x0 -> x2, Pallas kernels: none -> 114 us  [the longest x1 108 us: body(): pl.pallas_call(exchange_kernel, out_shape=(jax.ShapeDtypeStruct((N, ROWS,...]
    psum x4 -> x0, blocking collectives: 83 us -> none  [one_axis_at_a_time(): return functools.reduce(lax.psum, axes, x)]
    all_to_all x3 -> x0, waiting for transfers between devices: 71.5 us -> none  [the longest x1 49.8 us: body(): lax.all_to_all(raw_update, FSDP, split_axis=1, concat_axis=0, tiled=True)]
    all_to_all x1 -> x0, blocking collectives: 66.4 us -> none  [body(): lax.all_to_all(stat_rows, FSDP, split_axis=0, concat_axis=1, tiled=True)]
    all_to_all x3 -> x0, starting transfers between devices: 26.3 us -> none  [the longest x1 11.5 us: body(): lax.all_to_all(grad_rows, FSDP, split_axis=0, concat_axis=1, tiled=True)]
    gather x4 -> x0, local copies, waits for them, and re-layouts: 17.2 us -> none  [the longest x1 5.02 us: body(): stat_rows = jnp.take(statistics, placed, axis=0)]
    unnamed x12 -> x0, local copies, waits for them, and re-layouts: 10.4 us -> none
  transfers between devices with their start and end apart: 3 -> 0, of which waited for: 2 -> 0; matrix products, arithmetic and copies ran while one was open for 6% -> 0% of each run, Pallas kernels for 0% -> 0%
where the time goes in v1:
time: 115 us
  Pallas kernels  114 us (99%)
    pallas_call x1, Pallas kernels, body(): pl.pallas_call(exchange_kernel, out_shape=(jax.ShapeDtypeStruct((N, ROWS,...  108 us
    pallas_call x1, Pallas kernels, body(): pl.pallas_call(output_kernel, out_shape=(jax.ShapeDtypeStruct((N, ROWS, B...  5.49 us

profile of v1, /device:TPU:1, one launch (start us, length us, event | category | flops | bytes accessed | tf_op | source)
XLA Modules:
  0.0 114.7 jit_solution(9092425659362903029)
XLA Ops:
  0.6 108.4 %exchange.1 = (f32[128,8,1024]{2,1,0:T(8,128)S(1)}, f32[1024,1024]{1,0:T(8,128)S(1)}, s16[128,8,1024]{2,1,0:T(8,128)(2,1)S(1)}, s16[128,8,1024]{2,1,0:T(8,128)(2,1)S(1)}, f32[128,1,128]{2,1,0:T(1,128)S(1)}) custom-call(s32[128]{0:T(128)} %slot.1, f32[128,8,1024]{2,1,0:T(8,128)} %stat_hbm.1, bf16[128,8,1024]{2,1,0:T(8,128)(2,1)} %grad_hbm.1), custom_call_target="tpu_custom_call" | custom-call | tf_op jit(solution)/shard_map/exchange/pallas_call | solution.py:511
  109.0 5.5 %outputs.1 = (f32[128,8,1024]{2,1,0:T(8,128)}, f32[1,1024,1024]{2,1,0:T(8,128)}, f32[128,8,1024]{2,1,0:T(8,128)}) custom-call(s32[128]{0:T(128)} %slot.1, f32[128,8,1024]{2,1,0:T(8,128)S(1)} %get-tuple-element.8.stat, f32[1024,1024]{1,0:T(8,128)S(1)} %get-tuple-element.9.root, s16[128,8,1024]{2,1,0:T(8,128)(2,1)S(1)} %get-tuple-element.10.outer, ...), custom_call_target="tpu_custom_call" | custom-call | tf_op jit(solution)/shard_map/outputs/pallas_call | solution.py:536

commit v2 on v1

--- a/solution.py
+++ b/solution.py
@@ -16,6 +16,7 @@
 BF16 = jnp.bfloat16
 I16 = jnp.int16
 I32 = jnp.int32
+F8 = jnp.float8_e4m3fn
 
 STAT_DECAY = 0.95
 RIDGE = 0.001
@@ -24,19 +25,23 @@
 PANEL = 256
 PANELS = B // PANEL
 TINY = 1e-30
+G_PIECES, S_PIECES, OUTER_PIECES, RAW_PIECES = 4, 1, 4, 2
 
 CHIPS = [o for o in itertools.product(range(4), repeat=3) if any(o)]
 HOPS = (0, 1, 2, 1)
 FAR_FIRST = sorted(CHIPS, key=lambda o: -sum(HOPS[k] for k in o))
-ROUND = [((2, 1, 3, 0)[j % 4], (5 * j + 3) % 16 // 4, (5 * j + 3) % 4) for j in range(16)]
-
-
-def quarter_code(x, inverse_max):
-    unit = x * inverse_max
-    a = jnp.abs(unit) + TINY
+ROUND = [(-(5 * j + 3) % 4, (5 * j + 3) % 16 // 4, (5 * j + 3) % 4) for j in range(16)]
+
+
+def quarter_scale(top):
+    return TOP * lax.rsqrt(top) * lax.rsqrt(lax.rsqrt(top))
+
+
+def quarter_code(x, scale):
+    a = jnp.abs(x) + TINY
     r = lax.rsqrt(a)
     s = lax.rsqrt(a * r)
-    return jnp.round(unit * r * s * TOP).astype(I32).astype(I16)
+    return jnp.round((x * r) * (s * scale)).astype(I32).astype(I16)
 
 
 def quarter_value(q, top_to_value):
@@ -79,6 +84,14 @@
     return put
 
 
+def put_both(full, narrow):
+    def put(rows, cols, value):
+        full[rows, cols] = value
+        narrow(rows, cols, value)
+
+    return put
+
+
 def put_split(high, low):
     def put(rows, cols, value):
         hi = value.astype(BF16)
@@ -88,9 +101,23 @@
     return put
 
 
+def put_eighths(high, near, low, scale):
+    def put(rows, cols, value):
+        hi = value.astype(BF16)
+        high[rows, cols] = hi
+        near[rows, cols] = (value * scale).astype(F8)
+        low[rows, cols] = ((value - hi.astype(F32)) * (scale * 256.0)).astype(F8)
+
+    return put
+
+
+def fold(tile):
+    return jnp.sum(tile.reshape(16, 8, 128), axis=0)
+
+
 def exchange_kernel(
     slot_hbm, stat_hbm, grad_hbm, stat, root, outer_in, raw_in, misc_in,
-    slots, placed_row, placed, gin, gsend, ssend, grecv, srecv, gm, nf, vf, nb, nl, sb, zb, vb, code, msend,
+    slots, placed_row, placed, gin, gsend, ssend, grecv, srecv, gm, nf, vf, nb, n8, l8, sb, zb, vb, code, msend,
     load_p, load_g, load_s, g_out, g_in, s_out, s_in, e_out, e_in, o_out, o_in, r_out, r_in, m_out, m_in,
 ):
     sf = root
@@ -113,15 +140,22 @@
             device_id={AXIS: target}, device_id_type=MESH,
         ).start()
 
+    def to_round(i, cores, go):
+        for j, (kx, kz, ky) in enumerate(ROUND):
+            for c in cores:
+                target = first_device(i, j) + c
+                if kz == 0 and ky == 0:
+                    pl.when(target != me)(lambda: go(target))
+                else:
+                    go(target)
+
+    def first_device(i, j):
+        kx, kz, ky = ROUND[j]
+        return lax.rem(x + kx + i, 4) * 32 + at_z[kz] + at_y[ky]
+
     def to_chips(cores, go):
         def step(i, carry):
-            for kx, kz, ky in ROUND:
-                chip = lax.rem(x + kx + i, 4) * 32 + at_z[kz] + at_y[ky]
-                for c in cores:
-                    if kz == 0 and ky == 0:
-                        pl.when(chip + c != me)(lambda: go(chip + c))
-                    else:
-                        go(chip + c)
+            to_round(i, cores, go)
             return carry
 
         lax.fori_loop(0, 4, step, 0)
@@ -177,24 +211,29 @@
     with jax.named_scope("wait_barrier"):
         pl.semaphore_wait(barrier, N - 1)
 
-    def send_g(target, half):
-        cols = pl.ds(512 * half, 512)
+    def pieces(count, width=B):
+        return [pl.ds(width // count * i, width // count) for i in range(count)]
+
+    def send_g(target, cols):
         send(gsend.at[target, :, cols], grecv.at[me, :, cols], g_out, g_in, target)
 
-    def send_s(target):
-        send(ssend.at[target, :, pl.ds(0, 512)], srecv.at[me, :, pl.ds(0, 512)], s_out, s_in, target)
-
+    def send_s(target, cols):
+        send(ssend.at[target, :, cols], srecv.at[me, :, cols], s_out, s_in, target)
+
+    def send_extra(target):
         @pl.when(lax.rem(target // 2, 2) == high)
         def _():
             send(ssend.at[target, :, pl.ds(512, 128)], srecv.at[me, :, pl.ds(512, 128)], e_out, e_in, target)
 
     for group in (0, 1):
         with jax.named_scope("send_g"):
-            for half in (0, 1):
-                to_chips((group,), lambda target: send_g(target, half))
+            for cols in pieces(G_PIECES):
+                to_chips((group,), lambda target: send_g(target, cols))
         pack_s(group)
         with jax.named_scope("send_s"):
-            to_chips((group,), send_s)
+            for cols in pieces(S_PIECES, 512):
+                to_chips((group,), lambda target: send_s(target, cols))
+            to_chips((group,), send_extra)
 
     grecv[me] = gsend[me]
     srecv[me] = ssend[me]
@@ -211,24 +250,36 @@
     def put_nf(rows, cols, value):
         nf[rows, cols] = value
 
-    def outer_product(p):
+    def outer_product(p, top):
         rows, cols = below(p)
         outer = lax.dot_general(gm[rows, :], gm[cols, :], (((1,), (1,)), ((), ())), preferred_element_type=F32)
-        mirror(p, outer * (1.0 - STAT_DECAY), put_nf)
-
-    def outer_panel(p, tops):
-        rows = pl.ds(p * PANEL, PANEL)
-        outer = nf[rows, :]
-        top = jnp.maximum(jnp.max(jnp.abs(outer), keepdims=True), TINY)
-        code[pl.ds(p * 32, 32)] = quarter_code(outer, 1.0 / top).reshape(32, ROWS, B)
-        return jnp.where(lane == p, top, tops)
+        outer = outer * (1.0 - STAT_DECAY)
+        mirror(p, outer, put_nf)
+        return jnp.maximum(top, jnp.max(outer[:, :PANEL], axis=0, keepdims=True))
+
+    def outer_panel(p, scale):
+        code[pl.ds(p * 32, 32)] = quarter_code(nf[pl.ds(p * PANEL, PANEL), :], scale).reshape(32, ROWS, B)
+        return scale
+
+    def send_outer():
+        for cols in pieces(OUTER_PIECES):
+            to_chips(
+                (0, 1), lambda target: send(code.at[target, :, cols], outer_in.at[me, :, cols], o_out, o_in, target)
+            )
 
     with jax.named_scope("outer"):
         lax.fori_loop(0, PANELS, unpack_g, 0)
+        outer_top = jnp.full((1, PANEL), TINY, F32)
         for p in range(PANELS):
-            outer_product(p)
+            outer_top = outer_product(p, outer_top)
+        outer_top = jnp.max(outer_top, keepdims=True)
     with jax.named_scope("outer_code"):
-        outer_tops = lax.fori_loop(0, PANELS, outer_panel, jnp.zeros((1, 128), F32))
+        lax.fori_loop(0, PANELS, outer_panel, quarter_scale(outer_top), unroll=2)
+
+    @pl.when(core == 1)
+    def _():
+        with jax.named_scope("send_outer"):
+            send_outer()
 
     eye = eye_block()
 
@@ -237,9 +288,9 @@
         return span, nf[span, span]
 
     def trace_step(i, total):
-        return total + diagonal(i)[1] * eye
-
-    zeros = jnp.zeros((128, 128), F32)
+        return total + fold(diagonal(i)[1] * eye)
+
+    zeros = jnp.zeros((8, 128), F32)
     grad_sq = jnp.sum(lax.fori_loop(0, 8, trace_step, zeros), keepdims=True) / (1.0 - STAT_DECAY)
 
     def wait_extra(count, out):
@@ -264,7 +315,8 @@
         wait_extras(False)
 
     stat_value = STAT_DECAY / stat_scale**2
-    put_n = put_split(nb, nl)
+    first_scale = 256.0 / (STAT_MAX + outer_top)
+    put_n = put_eighths(nb, n8, l8, first_scale)
 
     def add_tile(i, j, square, own):
         other = lax.rem(i + j, 8)
@@ -275,11 +327,11 @@
         nf[rows, cols] = value
         put_n(rows, cols, value)
         if own:
-            return square + value * value
+            return square + fold(value * value)
         mirrored = value.T
         nf[cols, rows] = mirrored
         put_n(cols, rows, mirrored)
-        return square + 2.0 * (value * value)
+        return square + 2.0 * fold(value * value)
 
     def tiles(i, square):
         for j in range(4):
@@ -287,8 +339,8 @@
         return square
 
     with jax.named_scope("tiles"):
-        square = lax.fori_loop(0, 8, tiles, zeros)
-        square = lax.fori_loop(0, 4, lambda i, acc: add_tile(i + 4 * bit, 4, acc, False), square)
+        square = lax.fori_loop(0, 8, tiles, zeros, unroll=2)
+        square = lax.fori_loop(0, 4, lambda i, acc: add_tile(i + 4 * bit, 4, acc, False), square, unroll=4)
         total_sq = jnp.sum(square, keepdims=True)
         trace = jnp.sum(lax.fori_loop(0, 8, trace_step, zeros), keepdims=True)
         mean = trace * (1.0 / B)
@@ -306,25 +358,20 @@
 
         lax.fori_loop(0, 8, center, 0)
 
-    def send_outer():
-        for half in (0, 1):
-            cols = pl.ds(512 * half, 512)
-            to_chips(
-                (0, 1), lambda target: send(code.at[target, :, cols], outer_in.at[me, :, cols], o_out, o_in, target)
-            )
-
-    def iterate(first, k, mu, scale_y, v_unit):
+    def iterate(first, k, mu, scale_y, v_unit, scale):
         phi = (5.0 - mu) * 0.25
         phi2 = phi * phi
         phi3 = phi2 * phi
         phi4 = phi2 * phi2
         quarter_y = scale_y * 0.25
         quarter_v = v_unit * 0.25
+        unscale = (1.0 / 256.0) / (scale * scale)
         with jax.named_scope("square"):
             for p in range(PANELS):
                 rows, cols = below(p)
                 hi = nb[rows, :]
-                s = product(hi, nb[:, cols]) + product(hi, nl[:, cols]) + product(nl[rows, :], nb[:, cols])
+                s = product(n8[rows, :], l8[:, cols]) + product(l8[rows, :], n8[:, cols])
+                s = product(hi, nb[:, cols]) + s * unscale
                 if first:
                     s = s * (shrink * shrink)
                     vf[rows, cols] = nf[rows, cols] * (shrink * -0.25)
@@ -332,8 +379,7 @@
                 else:
                     vn = product(vb[k, rows, :], nb[:, cols])
                     v = vf[rows, cols] * phi - nf[rows, cols] * quarter_y - vn * quarter_v
-                    vf[rows, cols] = v
-                    mirror(p, v, put_bf16(vb.at[1 - k]))
+                    mirror(p, v, put_both(vf, put_bf16(vb.at[1 - k])))
                 sf[rows, cols] = s
                 mirror(p, s, put_bf16(sb))
         n_n = phi4 - mu * phi3
@@ -354,91 +400,88 @@
             for p in range(PANELS):
                 rows, cols = below(p)
                 n = nf[rows, cols] + product(sb[rows, :], zb[:, cols])
-                nf[rows, cols] = n
-                mirror(p, n, put_n)
+                mirror(p, n, put_both(nf, put_eighths(nb, n8, l8, 256.0)))
         return phi4 * mu, scale_y * phi
 
     one = jnp.ones((1, 1), F32)
-    mu, scale_y = iterate(True, 0, shrink * mean * (1.0 + RIDGE), one, one)
-    with jax.named_scope("send_outer"):
-        send_outer()
-        outer_in[me] = code[me]
+    @pl.when(core == 0)
+    def _():
+        with jax.named_scope("send_outer"):
+            send_outer()
+
+    mu, scale_y = iterate(True, 0, shrink * mean * (1.0 + RIDGE), one, one, first_scale)
+
+    outer_in[me] = code[me]
 
     def later(k, carry):
         mu, scale_y, v_unit = carry
-        mu, scale_y = iterate(False, lax.rem(k, 2), mu, scale_y, v_unit)
+        mu, scale_y = iterate(False, lax.rem(k, 2), mu, scale_y, v_unit, 256.0)
         return mu, scale_y, one
 
     mu, scale_y, _ = lax.fori_loop(1, 3, later, (mu, scale_y, shrink * -0.25))
     phi = (5.0 - mu) * 0.25
     diag_root = root_scale * scale_y * phi
-    put_raw = put_split(sb, zb)
-
-    def put_root(rows, cols, value):
-        root[rows, cols] = value
-        put_raw(rows, cols, value)
-
-    def root_panel(p):
-        rows, cols = below(p)
-        v = vf[rows, cols] * phi - nf[rows, cols] * (scale_y * 0.25) - product(vb[1, rows, :], nb[:, cols]) * 0.25
-        mirror(p, v * root_scale, put_root)
-
-    def root_diagonal(i, carry):
-        span = pl.ds(pl.multiple_of(i * 128, 128), 128)
-        put_root(span, span, root[span, span] + eye * diag_root)
-        return carry
-
-    with jax.named_scope("root"):
-        for p in range(PANELS):
-            root_panel(p)
-        lax.fori_loop(0, 8, root_diagonal, 0)
-
     front = pl.ds(0, N - 1)
     pltpu.make_async_copy(code.at[front], outer_in.at[front], o_out).wait()
 
-    def raw_product(p):
-        rows = pl.ds(p * PANEL, PANEL)
-        raw = product(sb[rows, :], gm[...]) + product(zb[rows, :], gm[...])
-        vf[rows, :] = raw
+    chips = range(len(ROUND))
+    low_lane = lax.broadcasted_iota(I32, (16, 128), 1) - lax.broadcasted_iota(I32, (16, 128), 0)
+    put_parts = put_split(sb, zb)
+
+    def strips(i):
+        return [pl.ds(pl.multiple_of(first_device(i, j) * ROWS, 16), 16) for j in chips]
+
+    def gathered(ref, rows):
+        return jnp.concatenate([ref[r, :] for r in rows], axis=0)
+
+    def root_batch(i):
+        rows = strips(i)
+        batch = pl.ds(pl.multiple_of(i * PANEL, PANEL), PANEL)
+        vn = product(gathered(vb.at[1], rows), nb[...])
+        value = (gathered(vf, rows) * phi - gathered(nf, rows) * (scale_y * 0.25) - vn * 0.25) * root_scale
+        put_parts(batch, slice(None), value)
+        for j in chips:
+            device = first_device(i, j)
+            cols = pl.ds(pl.multiple_of(device // 16 * 128, 128), 128)
+            root[rows[j], :] = value[16 * j : 16 * (j + 1)]
+            tile = root[rows[j], cols] + jnp.where(low_lane == lax.rem(device, 16) * ROWS, diag_root, 0.0)
+            root[rows[j], cols] = tile
+            put_parts(pl.ds(pl.multiple_of(i * PANEL + 16 * j, 16), 16), cols, tile)
+
+    def raw_batch(i):
+        batch = pl.ds(pl.multiple_of(i * PANEL, PANEL), PANEL)
+        raw = product(sb[batch, :], gm[...]) + product(zb[batch, :], gm[...])
+        for j, r in zip(chips, strips(i)):
+            vf[r, :] = raw[16 * j : 16 * (j + 1)]
         return jnp.sum(raw * raw, keepdims=True), jnp.maximum(jnp.max(jnp.abs(raw), keepdims=True), TINY)
 
-    def raw_send(p, top):
-        rows = pl.ds(p * PANEL, PANEL)
-        code[pl.ds(p * 32, 32)] = quarter_code(vf[rows, :], 1.0 / top).reshape(32, ROWS, B)
-        for j in range(16):
-            k = (5 * j + 3) % 16
-            for half in (0, 1):
-                for c in (0, 1):
-                    cols = pl.ds(512 * half, 512)
-                    target = p * 32 + at_z[k // 4] + at_y[k % 4] + c
-
-                    def go():
-                        send(code.at[target, :, cols], raw_in.at[me, :, cols], r_out, r_in, target)
-
-                    if k == 0:
-                        pl.when(target != me)(go)
-                    else:
-                        go()
-
-    def panel_at(i):
-        half = i // 2
-        return lax.rem(x + 2 + half - lax.rem(i, 2) * (1 + 2 * half), 4)
-
-    def raw_panel(i, carry):
-        raw_sq, top, tops = carry
-        p = panel_at(i)
-        more, later = raw_product(p)
-        raw_send(panel_at(i - 1), top)
-        return raw_sq + more, later, jnp.where(lane == p, later, tops)
-
+    def raw_code(i, top):
+        scale = quarter_scale(top)
+        for j, r in zip(chips, strips(i)):
+            code[pl.ds(first_device(i, j), 2)] = quarter_code(vf[r, :], scale).reshape(2, ROWS, B)
+
+    def raw_send(i):
+        for cols in pieces(RAW_PIECES):
+            to_round(
+                i, (0, 1), lambda target: send(code.at[target, :, cols], raw_in.at[me, :, cols], r_out, r_in, target)
+            )
+
+    def finish(i, carry, last=False):
+        raw_sq, tops = carry
+        more, top = raw_batch(i)
+        if not last:
+            root_batch(i + 1)
+        raw_code(i, top)
+        raw_send(i)
+        return raw_sq + more, jnp.where(lane == i, top, tops)
+
+    with jax.named_scope("root"):
+        root_batch(0)
     with jax.named_scope("raw"):
-        raw_sq, top = raw_product(panel_at(0))
-        raw_sq, top, raw_tops = lax.fori_loop(
-            1, PANELS, raw_panel, (raw_sq, top, jnp.where(lane == panel_at(0), top, 0.0))
-        )
-        raw_send(panel_at(PANELS - 1), top)
-
-    tops = (raw_tops + pltpu.roll(outer_tops, 4, 1)) * (1.0 / TOP**4)
+        carry = lax.fori_loop(0, 3, finish, (jnp.zeros((1, 1), F32), jnp.zeros((1, 128), F32)))
+        raw_sq, raw_tops = finish(3, carry, last=True)
+
+    tops = (raw_tops + jnp.where(lane == 4, outer_top, 0.0)) * (1.0 / TOP**4)
     msend[...] = tops + jnp.where(lane == 8, grad_sq, 0.0) + jnp.where(lane == 9, raw_sq, 0.0)
     with jax.named_scope("send_m"):
         to_chips((0, 1), lambda target: send(msend, misc_in.at[me], m_out, m_in, target))
@@ -463,7 +506,9 @@
 ):
     put_root = pltpu.make_async_copy(root, root_out.at[0], root_sem)
     put_root.start()
-    panel = lax.axis_index(AXIS) // 32
+    me = lax.axis_index(AXIS)
+    source = lax.broadcasted_iota(I32, (N, 1, 1), 0)
+    turn = lax.rem(8 + me // 32 - source // 32 + lax.rem(me // 2, 4) - lax.rem(source // 2, 4), 4)
     lane = lax.broadcasted_iota(I32, (1, 1, 128), 2)
 
     def pick(v, at):
@@ -472,8 +517,8 @@
     values = misc[...]
     totals = jnp.sum(values, axis=0, keepdims=True)
     graft = jnp.sqrt(pick(totals, 8)) / jnp.sqrt(pick(totals, 9))
-    rscale[...] = jnp.broadcast_to(pick(values, panel) * graft, (N, 1, 128))
-    oscale[...] = jnp.broadcast_to(pick(values, panel + 4), (N, 1, 128))
+    rscale[...] = jnp.broadcast_to(pick(values, turn) * graft, (N, 1, 128))
+    oscale[...] = jnp.broadcast_to(pick(values, 4), (N, 1, 128))
     step = 8
 
     def chunk(i, carry):
@@ -524,7 +569,7 @@
             V((N, ROWS, B), BF16), V((N, ROWS, B), BF16), V((N, ROWS, 640), I16),
             V((N, ROWS, B), BF16), V((N, ROWS, 640), I16), V((B, B), BF16),
             V((B, B), F32), V((B, B), F32),
-            V((B, B), BF16), V((B, B), BF16), V((B, B), BF16), V((B, B), BF16), V((2, B, B), BF16),
+            V((B, B), BF16), V((B, B), F8), V((B, B), F8), V((B, B), BF16), V((B, B), BF16), V((2, B, B), BF16),
             V((N, ROWS, B), I16), V((1, 128), F32),
         ]
         + [dma] * 15,

time: 115 us -> 108 us (0.939)
  Pallas kernels: 114 us -> 107 us
    pallas_call x1, Pallas kernels: 108 us -> 101 us  [body(): pl.pallas_call(exchange_kernel, out_shape=(jax.ShapeDtypeStruct((N, ROWS,...]
where the time goes in v2:
time: 108 us; the launch traced here: 107 us
  Pallas kernels  107 us (99%)
    pallas_call x1, Pallas kernels, body(): pl.pallas_call(exchange_kernel, out_shape=(jax.ShapeDtypeStruct((N, ROWS,...  101 us
    pallas_call x1, Pallas kernels, body(): pl.pallas_call(output_kernel, out_shape=(jax.ShapeDtypeStruct((N, ROWS, B...  5.49 us

profile of v2, /device:TPU:1, one launch (start us, length us, event | category | flops | bytes accessed | tf_op | source)
XLA Modules:
  0.0 107.5 jit_solution(6319890815184805321)
XLA Ops:
  0.6 101.1 %exchange.1 = (f32[128,8,1024]{2,1,0:T(8,128)S(1)}, f32[1024,1024]{1,0:T(8,128)S(1)}, s16[128,8,1024]{2,1,0:T(8,128)(2,1)S(1)}, s16[128,8,1024]{2,1,0:T(8,128)(2,1)S(1)}, f32[128,1,128]{2,1,0:T(1,128)S(1)}) custom-call(s32[128]{0:T(128)} %slot.1, f32[128,8,1024]{2,1,0:T(8,128)} %stat_hbm.1, bf16[128,8,1024]{2,1,0:T(8,128)(2,1)} %grad_hbm.1), custom_call_target="tpu_custom_call" | custom-call | tf_op jit(solution)/shard_map/exchange/pallas_call | solution.py:556
  101.8 5.5 %outputs.1 = (f32[128,8,1024]{2,1,0:T(8,128)}, f32[1,1024,1024]{2,1,0:T(8,128)}, f32[128,8,1024]{2,1,0:T(8,128)}) custom-call(s32[128]{0:T(128)} %slot.1, f32[128,8,1024]{2,1,0:T(8,128)S(1)} %get-tuple-element.8.stat, f32[1024,1024]{1,0:T(8,128)S(1)} %get-tuple-element.9.root, s16[128,8,1024]{2,1,0:T(8,128)(2,1)S(1)} %get-tuple-element.10.outer, ...), custom_call_target="tpu_custom_call" | custom-call | tf_op jit(solution)/shard_map/outputs/pallas_call | solution.py:581

commit v3 on v2

--- a/solution.py
+++ b/solution.py
@@ -21,6 +21,7 @@
 STAT_DECAY = 0.95
 RIDGE = 0.001
 STAT_MAX = 200.0
+OUTER_MAX = (1.0 - 0.95) * 1024 * 24.0**2 * 1.01
 TOP = 32760.0
 PANEL = 256
 PANELS = B // PANEL
@@ -47,6 +48,21 @@
 def quarter_value(q, top_to_value):
     y = q.astype(I32).astype(F32)
     return (y * y) * (y * jnp.abs(y)) * top_to_value
+
+
+def eighth_code(x):
+    a = jnp.abs(x) + TINY
+    r = lax.rsqrt(a)
+    half = a * r
+    s = lax.rsqrt(half)
+    u = lax.rsqrt(half * s)
+    return jnp.round((x * r) * (s * u) * (TOP / OUTER_MAX**0.125)).astype(I32).astype(I16)
+
+
+def eighth_value(q):
+    y = q.astype(I32).astype(F32) * (1.0 / TOP)
+    y2 = y * y
+    return ((y2 * y2) * y2) * ((y * jnp.abs(y)) * OUTER_MAX)
 
 
 def half_code(x, scale):
@@ -116,9 +132,9 @@
 
 
 def exchange_kernel(
-    slot_hbm, stat_hbm, grad_hbm, stat, root, outer_in, raw_in, misc_in,
-    slots, placed_row, placed, gin, gsend, ssend, grecv, srecv, gm, nf, vf, nb, n8, l8, sb, zb, vb, code, msend,
-    load_p, load_g, load_s, g_out, g_in, s_out, s_in, e_out, e_in, o_out, o_in, r_out, r_in, m_out, m_in,
+    slot_hbm, stat_hbm, grad_hbm, stat, root, raw_in, misc_in,
+    slots, placed_row, placed, slot_of, outer_in, gin, gsend, ssend, grecv, srecv, gm, nf, vf, nb, n8, l8, sb, zb, vb, code, msend,
+    load_p, load_o, load_g, load_s, g_out, g_in, s_out, s_in, e_out, e_in, o_out, o_in, r_out, r_in, m_out, m_in,
 ):
     sf = root
     me = lax.axis_index(AXIS)
@@ -184,7 +200,10 @@
         )
         put_p = pltpu.make_async_copy(placed_row, placed, load_p)
         put_p.start()
+        put_o = pltpu.make_async_copy(slots, slot_of, load_o)
+        put_o.start()
         get_g.wait()
+        put_o.wait()
         put_p.wait()
 
     def pack_g(s, carry):
@@ -257,9 +276,9 @@
         mirror(p, outer, put_nf)
         return jnp.maximum(top, jnp.max(outer[:, :PANEL], axis=0, keepdims=True))
 
-    def outer_panel(p, scale):
-        code[pl.ds(p * 32, 32)] = quarter_code(nf[pl.ds(p * PANEL, PANEL), :], scale).reshape(32, ROWS, B)
-        return scale
+    def outer_panel(p, carry):
+        code[pl.ds(p * 32, 32)] = eighth_code(nf[pl.ds(p * PANEL, PANEL), :]).reshape(32, ROWS, B)
+        return carry
 
     def send_outer():
         for cols in pieces(OUTER_PIECES):
@@ -274,7 +293,7 @@
             outer_top = outer_product(p, outer_top)
         outer_top = jnp.max(outer_top, keepdims=True)
     with jax.named_scope("outer_code"):
-        lax.fori_loop(0, PANELS, outer_panel, quarter_scale(outer_top), unroll=2)
+        lax.fori_loop(0, PANELS, outer_panel, 0, unroll=2)
 
     @pl.when(core == 1)
     def _():
@@ -466,11 +485,15 @@
                 i, (0, 1), lambda target: send(code.at[target, :, cols], raw_in.at[me, :, cols], r_out, r_in, target)
             )
 
+    def turn_at(i):
+        return i + i // 2 - 2 * (i // 3)
+
     def finish(i, carry, last=False):
         raw_sq, tops = carry
+        i, following = turn_at(i), turn_at(i + 1)
         more, top = raw_batch(i)
         if not last:
-            root_batch(i + 1)
+            root_batch(following)
         raw_code(i, top)
         raw_send(i)
         return raw_sq + more, jnp.where(lane == i, top, tops)
@@ -481,31 +504,36 @@
         carry = lax.fori_loop(0, 3, finish, (jnp.zeros((1, 1), F32), jnp.zeros((1, 128), F32)))
         raw_sq, raw_tops = finish(3, carry, last=True)
 
-    tops = (raw_tops + jnp.where(lane == 4, outer_top, 0.0)) * (1.0 / TOP**4)
-    msend[...] = tops + jnp.where(lane == 8, grad_sq, 0.0) + jnp.where(lane == 9, raw_sq, 0.0)
+    msend[...] = raw_tops * (1.0 / TOP**4) + jnp.where(lane == 8, grad_sq, 0.0) + jnp.where(lane == 9, raw_sq, 0.0)
     with jax.named_scope("send_m"):
         to_chips((0, 1), lambda target: send(msend, misc_in.at[me], m_out, m_in, target))
     misc_in[me] = msend[...]
     raw_in[me] = code[me]
 
+    with jax.named_scope("wait_o"):
+        pltpu.make_async_copy(code.at[front], outer_in.at[front], o_in).wait()
+
+    def renew(b, carry):
+        stat[b] = stat[b] * STAT_DECAY + eighth_value(outer_in[slot_of[0, b]])
+        return carry
+
+    with jax.named_scope("renew"):
+        lax.fori_loop(0, N, renew, 0, unroll=4)
     with jax.named_scope("wait_out"):
         pltpu.make_async_copy(gsend.at[front], grecv.at[front], g_out).wait()
         pltpu.make_async_copy(ssend.at[front, :, pl.ds(0, 512)], srecv.at[front, :, pl.ds(0, 512)], s_out).wait()
         wait_extras(True)
         pltpu.make_async_copy(code.at[front], raw_in.at[front], r_out).wait()
         pltpu.make_async_copy(misc_in.at[front], misc_in.at[front], m_out).wait()
-    with jax.named_scope("wait_o"):
-        pltpu.make_async_copy(code.at[front], outer_in.at[front], o_in).wait()
     with jax.named_scope("wait_r"):
         pltpu.make_async_copy(code.at[front], raw_in.at[front], r_in).wait()
         pltpu.make_async_copy(misc_in.at[front], misc_in.at[front], m_in).wait()
 
 
-def output_kernel(
-    slot, stat, root, outer, raw, misc, new_out, root_out, update_out, nbuf, tbuf, oscale, rscale, root_sem, out_sems
-):
-    put_root = pltpu.make_async_copy(root, root_out.at[0], root_sem)
-    put_root.start()
+def output_kernel(slot, stat, root, raw, misc, new_out, root_out, update_out, tbuf, rscale, sems, out_sems):
+    puts = [pltpu.make_async_copy(root, root_out.at[0], sems.at[0]), pltpu.make_async_copy(stat, new_out, sems.at[1])]
+    for c in puts:
+        c.start()
     me = lax.axis_index(AXIS)
     source = lax.broadcasted_iota(I32, (N, 1, 1), 0)
     turn = lax.rem(8 + me // 32 - source // 32 + lax.rem(me // 2, 4) - lax.rem(source // 2, 4), 4)
@@ -518,30 +546,26 @@
     totals = jnp.sum(values, axis=0, keepdims=True)
     graft = jnp.sqrt(pick(totals, 8)) / jnp.sqrt(pick(totals, 9))
     rscale[...] = jnp.broadcast_to(pick(values, turn) * graft, (N, 1, 128))
-    oscale[...] = jnp.broadcast_to(pick(values, 4), (N, 1, 128))
-    step = 8
+    step = 16
 
     def chunk(i, carry):
         part = pl.ds(i * step, step)
         for j in range(step):
             b = i * step + j
             s = slot[b]
-            o_value = oscale[s]
-            r_value = rscale[s]
+            value = rscale[s]
             for c in range(8):
                 cols = slice(128 * c, 128 * (c + 1))
-                nbuf[b, :, cols] = stat[b, :, cols] * STAT_DECAY + quarter_value(outer[s, :, cols], o_value)
-                tbuf[b, :, cols] = quarter_value(raw[s, :, cols], r_value)
-        pltpu.make_async_copy(nbuf.at[part], new_out.at[part], out_sems.at[0, i]).start()
-        pltpu.make_async_copy(tbuf.at[part], update_out.at[part], out_sems.at[1, i]).start()
+                tbuf[b, :, cols] = quarter_value(raw[s, :, cols], value)
+        pltpu.make_async_copy(tbuf.at[part], update_out.at[part], out_sems.at[i]).start()
         return carry
 
     lax.fori_loop(0, N // step, chunk, 0)
     for i in range(N // step):
         part = pl.ds(i * step, step)
-        pltpu.make_async_copy(nbuf.at[part], new_out.at[part], out_sems.at[0, i]).wait()
-        pltpu.make_async_copy(tbuf.at[part], update_out.at[part], out_sems.at[1, i]).wait()
-    put_root.wait()
+        pltpu.make_async_copy(tbuf.at[part], update_out.at[part], out_sems.at[i]).wait()
+    for c in puts:
+        c.wait()
 
 
 def body(statistics, gradient, block_slot):
@@ -553,28 +577,28 @@
     statistics = pltpu.with_memory_space_constraint(statistics, pltpu.HBM)
     gradient = pltpu.with_memory_space_constraint(gradient, pltpu.HBM)
     block_slot = pltpu.with_memory_space_constraint(block_slot, pltpu.HBM)
-    stat, root, outer_rows, raw_rows, misc = pl.pallas_call(
+    stat, root, raw_rows, misc = pl.pallas_call(
         exchange_kernel,
         out_shape=(
             jax.ShapeDtypeStruct((N, ROWS, B), F32),
             jax.ShapeDtypeStruct((B, B), F32),
             jax.ShapeDtypeStruct((N, ROWS, B), I16),
-            jax.ShapeDtypeStruct((N, ROWS, B), I16),
             jax.ShapeDtypeStruct((N, 1, 128), F32),
         ),
         in_specs=[in_hbm, in_hbm, in_hbm],
-        out_specs=(vmem,) * 5,
+        out_specs=(vmem,) * 4,
         scratch_shapes=[
-            V((1, 128), I32), V((1, 128), I32), pltpu.SMEM((1, 128), I32),
+            V((1, 128), I32), V((1, 128), I32), pltpu.SMEM((1, 128), I32), pltpu.SMEM((1, 128), I32),
+            V((N, ROWS, B), I16),
             V((N, ROWS, B), BF16), V((N, ROWS, B), BF16), V((N, ROWS, 640), I16),
             V((N, ROWS, B), BF16), V((N, ROWS, 640), I16), V((B, B), BF16),
             V((B, B), F32), V((B, B), F32),
             V((B, B), BF16), V((B, B), F8), V((B, B), F8), V((B, B), BF16), V((B, B), BF16), V((2, B, B), BF16),
             V((N, ROWS, B), I16), V((1, 128), F32),
         ]
-        + [dma] * 15,
+        + [dma] * 16,
         compiler_params=pltpu.CompilerParams(
-            collective_id=0, has_side_effects=True, vmem_limit_bytes=41 * 1024 * 1024
+            collective_id=0, has_side_effects=True, vmem_limit_bytes=43 * 1024 * 1024
         ),
         name="exchange",
     )(block_slot, statistics, gradient)
@@ -585,14 +609,14 @@
             jax.ShapeDtypeStruct((1, B, B), F32),
             jax.ShapeDtypeStruct((N, ROWS, B), F32),
         ),
-        in_specs=[smem, vmem, vmem, vmem, vmem, vmem],
+        in_specs=[smem, vmem, vmem, vmem, vmem],
         out_specs=(in_hbm, in_hbm, in_hbm),
         scratch_shapes=[
-            V((N, ROWS, B), F32), V((N, ROWS, B), F32), V((N, 1, 128), F32), V((N, 1, 128), F32), dma, dma((2, 16)),
+            V((N, ROWS, B), F32), V((N, 1, 128), F32), dma((2,)), dma((8,)),
         ],
         compiler_params=pltpu.CompilerParams(vmem_limit_bytes=16 * 1024 * 1024),
         name="outputs",
-    )(block_slot, stat, root, outer_rows, raw_rows, misc)
+    )(block_slot, stat, root, raw_rows, misc)
 
 
 def solution(mesh):

time: 108 us -> 106 us (0.981)
  Pallas kernels: 107 us -> 105 us
    pallas_call x1, Pallas kernels: 101 us -> 99.9 us  [body(): pl.pallas_call(exchange_kernel, out_shape=(jax.ShapeDtypeStruct((N, ROWS,...]
where the time goes in v3:
time: 106 us
  Pallas kernels  105 us (99%)
    pallas_call x1, Pallas kernels, body(): pl.pallas_call(exchange_kernel, out_shape=(jax.ShapeDtypeStruct((N, ROWS,...  99.9 us
    pallas_call x1, Pallas kernels, body(): pl.pallas_call(output_kernel, out_shape=(jax.ShapeDtypeStruct((N, ROWS, B...  5.31 us

profile of v3, /device:TPU:1, one launch (start us, length us, event | category | flops | bytes accessed | tf_op | source)
XLA Modules:
  0.0 106.0 jit_solution(4164643148710361570)
XLA Ops:
  0.6 99.9 %exchange.1 = (f32[128,8,1024]{2,1,0:T(8,128)S(1)}, f32[1024,1024]{1,0:T(8,128)S(1)}, s16[128,8,1024]{2,1,0:T(8,128)(2,1)S(1)}, f32[128,1,128]{2,1,0:T(1,128)S(1)}) custom-call(s32[128]{0:T(128)} %slot.1, f32[128,8,1024]{2,1,0:T(8,128)} %stat_hbm.1, bf16[128,8,1024]{2,1,0:T(8,128)(2,1)} %grad_hbm.1), custom_call_target="tpu_custom_call" | custom-call | tf_op jit(solution)/shard_map/exchange/pallas_call | solution.py:580
  100.5 5.3 %outputs.1 = (f32[128,8,1024]{2,1,0:T(8,128)}, f32[1,1024,1024]{2,1,0:T(8,128)}, f32[128,8,1024]{2,1,0:T(8,128)}) custom-call(s32[128]{0:T(128)} %slot.1, f32[128,8,1024]{2,1,0:T(8,128)S(1)} %get-tuple-element.7.stat, f32[1024,1024]{1,0:T(8,128)S(1)} %get-tuple-element.8.root, s16[128,8,1024]{2,1,0:T(8,128)(2,1)S(1)} %get-tuple-element.9.raw, ...), custom_call_target="tpu_custom_call" | custom-call | tf_op jit(solution)/shard_map/outputs/pallas_call | solution.py:605

commit v4 on v3

--- a/solution.py
+++ b/solution.py
@@ -485,6 +485,11 @@
                 i, (0, 1), lambda target: send(code.at[target, :, cols], raw_in.at[me, :, cols], r_out, r_in, target)
             )
 
+    def send_misc(raw_sq, raw_tops):
+        msend[...] = raw_tops * (1.0 / TOP**4) + jnp.where(lane == 8, grad_sq, 0.0) + jnp.where(lane == 9, raw_sq, 0.0)
+        with jax.named_scope("send_m"):
+            to_chips((0, 1), lambda target: send(msend, misc_in.at[me], m_out, m_in, target))
+
     def turn_at(i):
         return i + i // 2 - 2 * (i // 3)
 
@@ -495,18 +500,18 @@
         if not last:
             root_batch(following)
         raw_code(i, top)
+        raw_sq, tops = raw_sq + more, jnp.where(lane == i, top, tops)
+        if last:
+            send_misc(raw_sq, tops)
         raw_send(i)
-        return raw_sq + more, jnp.where(lane == i, top, tops)
+        return raw_sq, tops
 
     with jax.named_scope("root"):
         root_batch(0)
     with jax.named_scope("raw"):
         carry = lax.fori_loop(0, 3, finish, (jnp.zeros((1, 1), F32), jnp.zeros((1, 128), F32)))
-        raw_sq, raw_tops = finish(3, carry, last=True)
-
-    msend[...] = raw_tops * (1.0 / TOP**4) + jnp.where(lane == 8, grad_sq, 0.0) + jnp.where(lane == 9, raw_sq, 0.0)
-    with jax.named_scope("send_m"):
-        to_chips((0, 1), lambda target: send(msend, misc_in.at[me], m_out, m_in, target))
+        finish(3, carry, last=True)
+
     misc_in[me] = msend[...]
     raw_in[me] = code[me]
 

time: 106 us -> 106 us (level)
  no operation moved by 1% of the time
where the time goes in v4:
time: 106 us
  Pallas kernels  105 us (99%)
    pallas_call x1, Pallas kernels, body(): pl.pallas_call(exchange_kernel, out_shape=(jax.ShapeDtypeStruct((N, ROWS,...  99.4 us
    pallas_call x1, Pallas kernels, body(): pl.pallas_call(output_kernel, out_shape=(jax.ShapeDtypeStruct((N, ROWS, B...  5.31 us

profile of v4, /device:TPU:1, one launch (start us, length us, event | category | flops | bytes accessed | tf_op | source)
XLA Modules:
  0.0 105.5 jit_solution(14923735147838900017)
XLA Ops:
  0.6 99.4 %exchange.1 = (f32[128,8,1024]{2,1,0:T(8,128)S(1)}, f32[1024,1024]{1,0:T(8,128)S(1)}, s16[128,8,1024]{2,1,0:T(8,128)(2,1)S(1)}, f32[128,1,128]{2,1,0:T(1,128)S(1)}) custom-call(s32[128]{0:T(128)} %slot.1, f32[128,8,1024]{2,1,0:T(8,128)} %stat_hbm.1, bf16[128,8,1024]{2,1,0:T(8,128)(2,1)} %grad_hbm.1), custom_call_target="tpu_custom_call" | custom-call | tf_op jit(solution)/shard_map/exchange/pallas_call | solution.py:585
  100.0 5.3 %outputs.1 = (f32[128,8,1024]{2,1,0:T(8,128)}, f32[1,1024,1024]{2,1,0:T(8,128)}, f32[128,8,1024]{2,1,0:T(8,128)}) custom-call(s32[128]{0:T(128)} %slot.1, f32[128,8,1024]{2,1,0:T(8,128)S(1)} %get-tuple-element.7.stat, f32[1024,1024]{1,0:T(8,128)S(1)} %get-tuple-element.8.root, s16[128,8,1024]{2,1,0:T(8,128)(2,1)S(1)} %get-tuple-element.9.raw, ...), custom_call_target="tpu_custom_call" | custom-call | tf_op jit(solution)/shard_map/outputs/pallas_call | solution.py:610

commit v5 on v4

--- a/solution.py
+++ b/solution.py
@@ -479,8 +479,8 @@
         for j, r in zip(chips, strips(i)):
             code[pl.ds(first_device(i, j), 2)] = quarter_code(vf[r, :], scale).reshape(2, ROWS, B)
 
-    def raw_send(i):
-        for cols in pieces(RAW_PIECES):
+    def raw_send(i, count):
+        for cols in pieces(count):
             to_round(
                 i, (0, 1), lambda target: send(code.at[target, :, cols], raw_in.at[me, :, cols], r_out, r_in, target)
             )
@@ -503,7 +503,7 @@
         raw_sq, tops = raw_sq + more, jnp.where(lane == i, top, tops)
         if last:
             send_misc(raw_sq, tops)
-        raw_send(i)
+        raw_send(i, 2 * RAW_PIECES if last else RAW_PIECES)
         return raw_sq, tops
 
     with jax.named_scope("root"):

time: 106 us -> 106 us (level)
  no operation moved by 1% of the time
where the time goes in v5:
time: 106 us
  Pallas kernels  105 us (99%)
    pallas_call x1, Pallas kernels, body(): pl.pallas_call(exchange_kernel, out_shape=(jax.ShapeDtypeStruct((N, ROWS,...  99.6 us
    pallas_call x1, Pallas kernels, body(): pl.pallas_call(output_kernel, out_shape=(jax.ShapeDtypeStruct((N, ROWS, B...  5.31 us

profile of v5, /device:TPU:1, one launch (start us, length us, event | category | flops | bytes accessed | tf_op | source)
XLA Modules:
  0.0 105.7 jit_solution(10588076742178175355)
XLA Ops:
  0.6 99.6 %exchange.1 = (f32[128,8,1024]{2,1,0:T(8,128)S(1)}, f32[1024,1024]{1,0:T(8,128)S(1)}, s16[128,8,1024]{2,1,0:T(8,128)(2,1)S(1)}, f32[128,1,128]{2,1,0:T(1,128)S(1)}) custom-call(s32[128]{0:T(128)} %slot.1, f32[128,8,1024]{2,1,0:T(8,128)} %stat_hbm.1, bf16[128,8,1024]{2,1,0:T(8,128)(2,1)} %grad_hbm.1), custom_call_target="tpu_custom_call" | custom-call | tf_op jit(solution)/shard_map/exchange/pallas_call | solution.py:585
  100.2 5.3 %outputs.1 = (f32[128,8,1024]{2,1,0:T(8,128)}, f32[1,1024,1024]{2,1,0:T(8,128)}, f32[128,8,1024]{2,1,0:T(8,128)}) custom-call(s32[128]{0:T(128)} %slot.1, f32[128,8,1024]{2,1,0:T(8,128)S(1)} %get-tuple-element.7.stat, f32[1024,1024]{1,0:T(8,128)S(1)} %get-tuple-element.8.root, s16[128,8,1024]{2,1,0:T(8,128)(2,1)S(1)} %get-tuple-element.9.raw, ...), custom_call_target="tpu_custom_call" | custom-call | tf_op jit(solution)/shard_map/outputs/pallas_call | solution.py:610
